TPU v7x, 32 devices: a whole 2x2x4 slice. The times are simulated.
32 devices in a mesh: seq: 8 (over z, y), head: 4 (over x, core).
Axes of the slice: x: 2, y: 2, z: 4, core: 2. Of those that a mesh axis runs over, the one named last changes fastest.
Arguments:
- query: bfloat16 [512, 2048], P('seq', 'head'), may hold values from -16 to 16
- key_states: bfloat16 [512, 2048], P('seq', 'head'), may hold values from -16 to 16
- value_states: bfloat16 [512, 2048], P('seq', 'head'), may hold values from -6 to 6
- doc_ids: int32 [512], P('seq'), may hold values from 0 to 3, never falling along the last dimension, each value on 1 to 256 neighbouring positions
- out_weight: bfloat16 [2048, 4096], P('head', 'seq'), may hold values from -0.1875 to 0.1875
- residual: bfloat16 [512, 4096], P('seq', 'head'), may hold values from -6 to 6
Outputs:
- mixed: bfloat16 [512, 4096], P('seq', 'head')
Inputs may be any that keep to these rules, and one draw needn't show every extreme that they name: doc_ids never fall along the sequence; every document has 1 to 256 positions, and one has exactly 256.
All inputs are finite; a program needn't handle non-finite values.
Results may differ from a plain program's by a relative error of at most 0.0055.
Values may be sent and summed in bfloat16 or wider, within the bound.
A program may use at most 64 MiB of HBM per device.

v0:
```python
import functools

import jax
import jax.numpy as jnp
from jax import lax
from jax.experimental import pallas as pl
from jax.experimental.pallas import tpu as pltpu
from jax.sharding import PartitionSpec as P

HEAD_DIM = 128


masked_score = -1e30


def to_heads(block):
    return block.reshape(block.shape[0], block.shape[1] // HEAD_DIM, HEAD_DIM)


def attend_block(state, queries, query_pos, query_docs, keys, values, key_pos, key_docs):
    run_max, run_sum, run_acc = state
    scores = jnp.einsum(
        "qhd,khd->hqk", queries, keys, preferred_element_type=jnp.float32
    ) * HEAD_DIM ** (-0.5)
    allowed = (key_pos[None, :] <= query_pos[:, None]) & (key_docs[None, :] == query_docs[:, None])
    scores = jnp.where(allowed[None], scores, masked_score)
    new_max = jnp.maximum(run_max, jnp.max(scores, axis=-1))
    weights = jnp.where(allowed[None], jnp.exp(scores - new_max[..., None]), 0.0)
    run_sum = jnp.sum(weights, axis=-1)
    run_acc = jnp.einsum(
        "hqk,khd->hqd", weights.astype(jnp.bfloat16), values, preferred_element_type=jnp.float32
    )
    return (new_max, run_sum, run_acc)


def shards(query, key_states, value_states, doc_ids, out_weight, residual):
    tok_rows = query.shape[0]
    heads = query.shape[1] // HEAD_DIM
    shard_index = lax.axis_index("seq")
    first_pos = shard_index * tok_rows
    groups = [(query, first_pos + jnp.arange(tok_rows, dtype=jnp.int32), doc_ids)]
    prepared = [(to_heads(block), block_pos, block_docs) for block, block_pos, block_docs in groups]
    initial = tuple(
        (
            (
                jnp.full((heads, block_pos.shape[0]), masked_score, jnp.float32),
                jnp.zeros((heads, block_pos.shape[0]), jnp.float32),
                jnp.zeros((heads, block_pos.shape[0], HEAD_DIM), jnp.float32),
            )
            for block, block_pos, block_docs in groups
        )
    )
    first_row = jnp.int32(0)
    keys = lax.all_gather(key_states, "seq", axis=0, tiled=True)
    values = lax.all_gather(value_states, "seq", axis=0, tiled=True)
    key_docs = lax.all_gather(doc_ids, "seq", axis=0, tiled=True)
    key_pos = jnp.arange(keys.shape[0], dtype=jnp.int32)
    key_heads = to_heads(keys)
    value_heads = to_heads(values)
    updated = []
    for member, state in zip(prepared, initial):
        queries, query_pos, query_docs = member

        def advance(inner, queries=queries, query_pos=query_pos, query_docs=query_docs):
            return attend_block(
                inner, queries, query_pos, query_docs, key_heads, value_heads, key_pos, key_docs
            )

        def unchanged(inner):
            return inner

        updated.append(lax.cond(first_row <= jnp.max(query_pos), advance, unchanged, state))
    finals = tuple(updated)
    outputs = []
    for run_max, run_sum, run_acc in finals:
        normed = run_acc / run_sum[..., None]
        outputs.append(
            jnp.transpose(normed, (1, 0, 2))
            .reshape(normed.shape[1], heads * HEAD_DIM)
            .astype(jnp.bfloat16)
        )
    attended = outputs[0]
    mapped = jnp.dot(
        attended,
        lax.all_gather(out_weight, "seq", axis=1, tiled=True),
        preferred_element_type=jnp.float32,
    )
    summed = lax.psum_scatter(mapped, "head", scatter_dimension=1, tiled=True)
    return (residual.astype(jnp.float32) + summed).astype(jnp.bfloat16)


MESH = pl.DeviceIdType.MESH


CHUNKS = 2


def attention(queries, keys, values, doc_row, first_row, pos_rows):
    rows, keep = queries.shape[0], keys.shape[0]
    scores = lax.dot_general(
        queries, keys, (((1,), (1,)), ((), ())), preferred_element_type=jnp.float32
    ) * HEAD_DIM ** (-0.5)
    row_pos = lax.broadcasted_iota(jnp.int32, (rows, keep), 0) + first_row
    col_pos = lax.broadcasted_iota(jnp.int32, (rows, keep), 1)
    docs = jnp.broadcast_to(doc_row, (rows, keep))
    query_docs = jnp.sum(jnp.where(row_pos == col_pos, docs, 0), axis=1, keepdims=True)
    allowed = (col_pos <= row_pos) & (docs == query_docs)
    scores = jnp.where(allowed, scores, masked_score)
    row_max = jnp.max(scores, axis=1, keepdims=True)
    weights = jnp.where(allowed, jnp.exp(scores - row_max), 0.0)
    row_sum = jnp.sum(weights, axis=1, keepdims=True)
    product = jnp.dot(weights.astype(jnp.bfloat16), values, preferred_element_type=jnp.float32)
    return (product / row_sum).astype(jnp.bfloat16)


def fused_kernel(
    n, nh, q_ref, k_ref, v_ref, doc_ref, w_ref, res_ref, out_ref,
    qbuf, kbuf, vbuf, docbuf, att, wbuf, sendbuf, parts, resbuf,
    q_send, q_recv, k_send, k_recv, v_send, v_recv, d_send, d_recv,
    z_send, z_recv, f_send, f_recv, p_send, p_recv, w_sems, w_recv, res_sem,
):
    me = lax.axis_index("seq")
    head = lax.axis_index("head")
    rows = k_ref.shape[0]
    half = n // 2
    mid = half * rows
    plane, side = me // 2, me % 2
    my_half = me // half
    pair, core = head // 2, head % 2
    partner = pair * 2 + (1 - core)
    wrows, wcols = w_ref.shape
    w_slot = wbuf.at[pl.ds(pl.multiple_of(core * wrows, wrows), wrows), :]

    res_copy = pltpu.make_async_copy(res_ref, resbuf, res_sem)
    res_copy.start()

    barrier = pltpu.get_barrier_semaphore()
    for ds_ in range(n):
        for dh in range(nh):
            if ds_ == 0 and dh == 0:
                continue
            pl.semaphore_signal(
                barrier, inc=1,
                device_id=(lax.rem(me + ds_, n), lax.rem(head + dh, nh)),
                device_id_type=MESH,
            )
    pl.semaphore_wait(barrier, n * nh - 1)

    def block(ref, source):
        return ref.at[pl.ds(pl.multiple_of(source * rows, rows), rows), :]

    def lanes(ref, index):
        return ref.at[:, pl.ds(pl.multiple_of(index * HEAD_DIM, HEAD_DIM), HEAD_DIM)]

    def send_kv(kind, dst):
        src, dest, ssem, rsem = kind
        return pltpu.make_async_remote_copy(
            src_ref=lanes(src, dst // 2), dst_ref=block(dest, me),
            send_sem=ssem.at[dst], recv_sem=rsem.at[me],
            device_id=(dst, head), device_id_type=MESH,
        )

    def local_kv(kind):
        src, dest, ssem, rsem = kind
        return pltpu.make_async_copy(lanes(src, plane), block(dest, me), rsem.at[me])

    def send_q(dst):
        return pltpu.make_async_remote_copy(
            src_ref=lanes(q_ref, dst // 2), dst_ref=block(qbuf, me % half),
            send_sem=q_send.at[dst], recv_sem=q_recv.at[me % half],
            device_id=(dst, head), device_id_type=MESH,
        )

    def send_doc(dst):
        return pltpu.make_async_remote_copy(
            src_ref=doc_ref, dst_ref=docbuf.at[me],
            send_sem=d_send.at[dst], recv_sem=d_recv.at[me],
            device_id=(dst, head), device_id_type=MESH,
        )

    kinds = ((k_ref, kbuf, k_send, k_recv), (v_ref, vbuf, v_send, v_recv))

    for off in range(1, n):
        dst = lax.rem(me + off, n)

        @pl.when((dst % 2 == 1) | (my_half == 0))
        def _(dst=dst):
            send_kv(kinds[0], dst).start()

        @pl.when(dst % 2 == my_half)
        def _(dst=dst):
            send_q(dst).start()

        send_doc(dst).start()

        @pl.when((dst % 2 == 1) | (my_half == 0))
        def _(dst=dst):
            send_kv(kinds[1], dst).start()

    def w_send(to, sem):
        return pltpu.make_async_remote_copy(
            src_ref=w_ref, dst_ref=w_slot, send_sem=w_sems.at[sem], recv_sem=w_recv.at[core],
            device_id=to, device_id_type=MESH,
        )

    w_across = w_send((2 * plane + 1 - side, pair * 2 + side), 0)
    w_beside = w_send((me, partner), 1)
    w_across.start()

    @pl.when(core == side)
    def _():
        pltpu.make_async_copy(w_ref, w_slot, w_recv.at[core]).start()

    @pl.when(core != side)
    def _():
        w_beside.start()

    @pl.when((side == 1) | (my_half == 0))
    def _():
        for kind in kinds:
            local_kv(kind).start()

    @pl.when(side == my_half)
    def _():
        pltpu.make_async_copy(
            lanes(q_ref, plane), block(qbuf, me % half), q_recv.at[me % half]
        ).start()

    pltpu.make_async_copy(doc_ref, docbuf.at[me], d_recv.at[me]).start()

    def arrived(ref, sem):
        pltpu.make_async_copy(ref, ref, sem).wait()

    for source in range(n):
        arrived(docbuf.at[source], d_recv.at[source])
    for source in range(half):
        arrived(qbuf.at[pl.ds(source * rows, rows), :], q_recv.at[source])
        for _, dest, _, rsem in kinds:
            arrived(dest.at[pl.ds(source * rows, rows), :], rsem.at[source])

    doc_row = jnp.concatenate([docbuf[source] for source in range(n)], axis=1)

    @pl.when(side == 0)
    def _():
        att[core * half + plane] = attention(
            qbuf[...], kbuf[:mid, :], vbuf[:mid, :], doc_row[:, :mid], 0, mid
        )

    @pl.when(side == 1)
    def _():
        for source in range(half, n):
            for _, dest, _, rsem in kinds:
                arrived(dest.at[pl.ds(source * rows, rows), :], rsem.at[source])
        att[core * half + plane] = attention(
            qbuf[...], kbuf[...], vbuf[...], doc_row, mid, mid
        )

    chunk = mid // CHUNKS

    def att_chunk(c, source, part):
        start = part * chunk
        return att.at[
            c * half + source // 2, pl.ds(pl.multiple_of(start, chunk), chunk), :
        ]

    def att_copy(source, part, send, recv, to):
        ref = att_chunk(core, source, part)
        return pltpu.make_async_remote_copy(
            src_ref=ref, dst_ref=ref, send_sem=send, recv_sem=recv,
            device_id=to, device_id_type=MESH,
        )

    def along(dz, part):
        return att_copy(
            me, part, z_send.at[dz, part], z_recv.at[plane, part], (2 * dz + side, head)
        )

    def forward(source, part):
        return att_copy(
            source, part, f_send.at[source // 2, part], f_recv.at[source // 2, part], (me, partner)
        )

    offsets = list(range(1, half))
    near_first = sorted(offsets, key=lambda off: min(off, half - off))
    for off in reversed(near_first):
        for part in range(CHUNKS):
            along(lax.rem(plane + off, half), part).start()
    for part in range(CHUNKS):
        forward(me, part).start()

    for off in near_first:
        sz = lax.rem(plane + off, half)
        for part in range(CHUNKS):
            arrived(att_chunk(core, 2 * sz + side, part), z_recv.at[sz, part])
            forward(2 * sz + side, part).start()

    for slot in range(2):
        arrived(wbuf.at[pl.ds(slot * wrows, wrows), :], w_recv.at[slot])
    for sz in range(half):
        for part in range(CHUNKS):
            arrived(att_chunk(1 - core, 2 * sz + side, part), f_recv.at[sz, part])
    attended = jnp.concatenate([att[index] for index in range(n)], axis=1)
    sendbuf[...] = jnp.dot(
        attended, wbuf[...], preferred_element_type=jnp.float32
    ).astype(jnp.bfloat16)
    slot = pair * 2 + core
    for index in range(half):
        target = side * half + index
        src = sendbuf.at[pl.ds(index * rows, rows), :]
        own = (me == target) & (head == plane)

        @pl.when(own)
        def _(src=src):
            pltpu.make_async_copy(src, parts.at[slot], p_recv.at[slot]).start()

        @pl.when(jnp.logical_not(own))
        def _(src=src, target=target, index=index):
            pltpu.make_async_remote_copy(
                src_ref=src, dst_ref=parts.at[slot],
                send_sem=p_send.at[index], recv_sem=p_recv.at[slot],
                device_id=(target, plane), device_id_type=MESH,
            ).start()

    res_copy.wait()
    for c in range(2):
        for p in range(2):
            arrived(parts.at[2 * p + c], p_recv.at[2 * p + c])
        cols = slice(c * wcols, (c + 1) * wcols)
        total = parts[c].astype(jnp.float32) + parts[2 + c].astype(jnp.float32)
        out_ref[:, cols] = (resbuf[:, cols].astype(jnp.float32) + total).astype(jnp.bfloat16)

    for off in range(1, n):
        dst = lax.rem(me + off, n)

        @pl.when((dst % 2 == 1) | (my_half == 0))
        def _(dst=dst):
            for kind in kinds:
                send_kv(kind, dst).wait_send()

        @pl.when(dst % 2 == my_half)
        def _(dst=dst):
            send_q(dst).wait_send()

        send_doc(dst).wait_send()
    for part in range(CHUNKS):
        for off in near_first:
            along(lax.rem(plane + off, half), part).wait_send()
        for sz in range(half):
            forward(2 * sz + side, part).wait_send()
    w_across.wait_send()

    @pl.when(core != side)
    def _():
        w_beside.wait_send()

    for index in range(half):
        src = sendbuf.at[pl.ds(index * rows, rows), :]

        @pl.when(jnp.logical_not((me == side * half + index) & (head == plane)))
        def _(src=src, index=index):
            pltpu.make_async_copy(src, src, p_send.at[index]).wait()


def fused(n, nh, query, key_states, value_states, doc_ids, out_weight, residual):
    rows, width = key_states.shape
    wrows, wcols = out_weight.shape
    seq = n * rows
    dma = pltpu.SemaphoreType.DMA
    vmem = pl.BlockSpec(memory_space=pltpu.VMEM)
    any_ = pl.BlockSpec(memory_space=pl.ANY)
    bf16 = jnp.bfloat16
    return pl.pallas_call(
        functools.partial(fused_kernel, n, nh),
        out_shape=jax.ShapeDtypeStruct(residual.shape, residual.dtype),
        in_specs=[vmem, vmem, vmem, vmem, any_, any_],
        out_specs=vmem,
        scratch_shapes=[
            pltpu.VMEM((seq // 2, HEAD_DIM), bf16),
            pltpu.VMEM((seq, HEAD_DIM), bf16),
            pltpu.VMEM((seq, HEAD_DIM), bf16),
            pltpu.VMEM((n, 1, rows), jnp.int32),
            pltpu.VMEM((n, seq // 2, HEAD_DIM), bf16),
            pltpu.VMEM((2 * wrows, wcols), bf16),
            pltpu.VMEM((seq // 2, wcols), bf16),
            pltpu.VMEM((4, rows, wcols), bf16),
            pltpu.VMEM(residual.shape, bf16),
            dma((n,)), dma((n // 2,)),
            dma((n,)), dma((n,)),
            dma((n,)), dma((n,)),
            dma((n,)), dma((n,)),
            dma((n // 2, CHUNKS)), dma((n // 2, CHUNKS)),
            dma((n // 2, CHUNKS)), dma((n // 2, CHUNKS)),
            dma((n // 2,)), dma((4,)),
            dma((2,)), dma((2,)), dma,
        ],
        compiler_params=pltpu.CompilerParams(collective_id=0, has_side_effects=True),
    )(query, key_states, value_states, doc_ids.reshape(1, rows), out_weight, residual)


def solution(mesh):
    placed = (
        P("seq", "head"),
        P("seq", "head"),
        P("seq", "head"),
        P("seq"),
        P("head", "seq"),
        P("seq", "head"),
    )
    n, nh = mesh.shape["seq"], mesh.shape["head"]

    def body(query, key_states, value_states, doc_ids, out_weight, residual):
        heads = query.shape[1] // HEAD_DIM
        fits = (
            n == 2 * heads
            and n == 2 * nh
            and nh % 2 == 0
            and out_weight.shape[1] % 256 == 0
            and query.shape[0] % 16 == 0
        )
        run = functools.partial(fused, n, nh) if fits else shards
        return run(query, key_states, value_states, doc_ids, out_weight, residual)

    return jax.shard_map(
        body, mesh=mesh, in_specs=placed, out_specs=P("seq", "head"), check_vma=False
    )
```

profile of v0, /device:TPU:25, one launch (start us, length us, event | category | flops | bytes accessed | tf_op | source)
XLA Modules:
  0.0 39.9 jit_solution(5225403582056419137)
XLA Ops:
  0.0 38.3 %shard_map.64 = bf16[64,1024]{1,0:T(8,128)(2,1)} custom-call(bf16[64,512]{1,0:T(8,128)(2,1)} %q_ref.1, bf16[64,512]{1,0:T(8,128)(2,1)} %k_ref.1, bf16[64,512]{1,0:T(8,128)(2,1)} %v_ref.1, s32[1,64]{1,0:T(1,128)} %bitcast.1, bf16[512,512]{1,0:T(8,128)(2,1)} %w_ref.1, bf16[64,1024]{1,0:T(8,128)(2,1)} %res_ref.1), custom_call_target="tpu_custom_call" | custom-call | tf_op jit(solution)/shard_map/pallas_call | solution.py:372
  38.3 1.6 %copy.8 = bf16[64,1024]{1,0:T(8,128)(2,1)} copy(bf16[64,1024]{1,0:T(8,128)(2,1)} %shard_map.64) | data formatting | bytes 262144
where the time goes:
time: 40 us; the launch traced here: 39.9 us
  Pallas kernels  38.3 us (96%)
  local copies, waits for them, and re-layouts  1.57 us (4%)
    pallas_call x1, Pallas kernels, fused(): pl.pallas_call(functools.partial(fused_kernel, n, nh), out_shape=jax.Shap...  38.3 us
    unnamed x1, local copies, waits for them, and re-layouts  1.57 us

commit v1 on v0

v1 whole, which is shorter than its diff:
```python
import functools

import jax
import jax.numpy as jnp
from jax import lax
from jax.experimental import pallas as pl
from jax.experimental.pallas import tpu as pltpu
from jax.sharding import PartitionSpec as P

HEAD_DIM = 128


masked_score = -1e30


def to_heads(block):
    return block.reshape(block.shape[0], block.shape[1] // HEAD_DIM, HEAD_DIM)


def attend_block(state, queries, query_pos, query_docs, keys, values, key_pos, key_docs):
    run_max, run_sum, run_acc = state
    scores = jnp.einsum(
        "qhd,khd->hqk", queries, keys, preferred_element_type=jnp.float32
    ) * HEAD_DIM ** (-0.5)
    allowed = (key_pos[None, :] <= query_pos[:, None]) & (key_docs[None, :] == query_docs[:, None])
    scores = jnp.where(allowed[None], scores, masked_score)
    new_max = jnp.maximum(run_max, jnp.max(scores, axis=-1))
    weights = jnp.where(allowed[None], jnp.exp(scores - new_max[..., None]), 0.0)
    run_sum = jnp.sum(weights, axis=-1)
    run_acc = jnp.einsum(
        "hqk,khd->hqd", weights.astype(jnp.bfloat16), values, preferred_element_type=jnp.float32
    )
    return (new_max, run_sum, run_acc)


def shards(query, key_states, value_states, doc_ids, out_weight, residual):
    tok_rows = query.shape[0]
    heads = query.shape[1] // HEAD_DIM
    shard_index = lax.axis_index("seq")
    first_pos = shard_index * tok_rows
    groups = [(query, first_pos + jnp.arange(tok_rows, dtype=jnp.int32), doc_ids)]
    prepared = [(to_heads(block), block_pos, block_docs) for block, block_pos, block_docs in groups]
    initial = tuple(
        (
            (
                jnp.full((heads, block_pos.shape[0]), masked_score, jnp.float32),
                jnp.zeros((heads, block_pos.shape[0]), jnp.float32),
                jnp.zeros((heads, block_pos.shape[0], HEAD_DIM), jnp.float32),
            )
            for block, block_pos, block_docs in groups
        )
    )
    first_row = jnp.int32(0)
    keys = lax.all_gather(key_states, "seq", axis=0, tiled=True)
    values = lax.all_gather(value_states, "seq", axis=0, tiled=True)
    key_docs = lax.all_gather(doc_ids, "seq", axis=0, tiled=True)
    key_pos = jnp.arange(keys.shape[0], dtype=jnp.int32)
    key_heads = to_heads(keys)
    value_heads = to_heads(values)
    updated = []
    for member, state in zip(prepared, initial):
        queries, query_pos, query_docs = member

        def advance(inner, queries=queries, query_pos=query_pos, query_docs=query_docs):
            return attend_block(
                inner, queries, query_pos, query_docs, key_heads, value_heads, key_pos, key_docs
            )

        def unchanged(inner):
            return inner

        updated.append(lax.cond(first_row <= jnp.max(query_pos), advance, unchanged, state))
    finals = tuple(updated)
    outputs = []
    for run_max, run_sum, run_acc in finals:
        normed = run_acc / run_sum[..., None]
        outputs.append(
            jnp.transpose(normed, (1, 0, 2))
            .reshape(normed.shape[1], heads * HEAD_DIM)
            .astype(jnp.bfloat16)
        )
    attended = outputs[0]
    mapped = jnp.dot(
        attended,
        lax.all_gather(out_weight, "seq", axis=1, tiled=True),
        preferred_element_type=jnp.float32,
    )
    summed = lax.psum_scatter(mapped, "head", scatter_dimension=1, tiled=True)
    return (residual.astype(jnp.float32) + summed).astype(jnp.bfloat16)


MESH = pl.DeviceIdType.MESH


STEPS = 2


def attention(queries, keys, values, doc_row, row_pos):
    rows, keep = queries.shape[0], keys.shape[0]
    scores = lax.dot_general(
        queries, keys, (((1,), (1,)), ((), ())), preferred_element_type=jnp.float32
    ) * HEAD_DIM ** (-0.5)
    col_pos = lax.broadcasted_iota(jnp.int32, (rows, keep), 1)
    docs = jnp.broadcast_to(doc_row, (rows, keep))
    query_docs = jnp.sum(jnp.where(row_pos == col_pos, docs, 0), axis=1, keepdims=True)
    allowed = (col_pos <= row_pos) & (docs == query_docs)
    scores = jnp.where(allowed, scores, masked_score)
    row_max = jnp.max(scores, axis=1, keepdims=True)
    weights = jnp.where(allowed, jnp.exp(scores - row_max), 0.0)
    row_sum = jnp.sum(weights, axis=1, keepdims=True)
    product = jnp.dot(weights.astype(jnp.bfloat16), values, preferred_element_type=jnp.float32)
    return (product / row_sum).astype(jnp.bfloat16)


def fused_kernel(
    nz, q_ref, k_ref, v_ref, doc_ref, w_ref, res_ref, out_ref,
    qin, kin, vin, docin, qbuf, kbuf, vbuf, docbuf, att, wbuf, sendbuf, parts, resbuf,
    in_sem, q_send, q_recv, k_send, k_recv, v_send, v_recv, d_send, d_recv,
    z_send, z_recv, f_send, f_recv, p_send, p_recv, w_send, w_recv, res_sem, near,
):
    me = lax.axis_index("seq")
    head = lax.axis_index("head")
    rows = k_ref.shape[0]
    z, y = me // 2, me % 2
    x, core = head // 2, head % 2
    wrows = w_ref.shape[0]
    wcols = w_ref.shape[1]

    barrier = pltpu.get_barrier_semaphore()

    def greet(sem, to):
        pl.semaphore_signal(sem, inc=1, device_id=to, device_id_type=MESH)

    def beside(far, act):
        for side, step in enumerate((-far, far)):
            @pl.when((z + step >= 0) & (z + step < nz))
            def _(side=side, step=step):
                act(side, z + step)

    beside(1, lambda side, to: greet(barrier, (2 * to + y, head)))
    for dy in range(2):
        for dh in range(4):
            if dy or dh:
                greet(barrier, (2 * z + lax.rem(y + dy, 2), lax.rem(head + dh, 4)))

    def lanes(ref, index):
        return ref.at[:, pl.ds(pl.multiple_of(index * HEAD_DIM, HEAD_DIM), HEAD_DIM)]

    def block(ref, index):
        return ref.at[pl.ds(pl.multiple_of(index * rows, rows), rows), :]

    kinds = ((kin, kbuf, k_send, k_recv), (vin, vbuf, v_send, v_recv))
    staged = [
        pltpu.make_async_copy(src, dst, in_sem.at[index])
        for index, (src, dst) in enumerate(
            ((k_ref, kin), (v_ref, vin), (q_ref, qin), (doc_ref, docin))
        )
    ]
    for copy in staged:
        copy.start()
    for src, (_, dst, _, recv) in zip((k_ref, v_ref), kinds):
        pltpu.make_async_copy(lanes(src, z), block(dst, me), recv.at[me]).start()
    pltpu.make_async_copy(lanes(q_ref, z), block(qbuf, z), q_recv.at[z]).start()
    pltpu.make_async_copy(doc_ref, docbuf.at[me], d_recv.at[me]).start()
    res_copy = pltpu.make_async_copy(res_ref, resbuf, res_sem)
    res_copy.start()

    w_slot = wbuf.at[pl.ds(pl.multiple_of(core * wrows, wrows), wrows), :]

    @pl.when(core == y)
    def _():
        pltpu.make_async_copy(w_ref, w_slot, w_recv.at[core]).start()

    pl.semaphore_wait(
        barrier, 7 + (z > 0).astype(jnp.int32) + (z < nz - 1).astype(jnp.int32)
    )

    def relay(turn):
        beside(1, lambda side, to: greet(near.at[turn, 1 - side], (2 * to + y, head)))

    def relayed(turn):
        beside(1, lambda side, to: pl.semaphore_wait(near.at[turn, side], 1))

    def arrived(ref, sem):
        pltpu.make_async_copy(ref, ref, sem).wait()

    def remote(src, dst, send, recv, to):
        return pltpu.make_async_remote_copy(
            src_ref=src, dst_ref=dst, send_sem=send, recv_sem=recv,
            device_id=to, device_id_type=MESH,
        )

    def send_kv(kind, to):
        src, dst, send, recv = kind
        return remote(
            lanes(src, to // 2), block(dst, me), send.at[to], recv.at[me], (to, head)
        )

    def send_q(to):
        return remote(
            lanes(qin, to // 2), block(qbuf, z), q_send.at[to], q_recv.at[z], (to, head)
        )

    def send_doc(to):
        return remote(docin, docbuf.at[me], d_send.at[to], d_recv.at[me], (to, head))

    def own_column(to):
        return [send_doc(to), send_kv(kinds[0], to), send_q(to), send_kv(kinds[1], to)]

    def other_column(to):
        return [send_doc(to), send_kv(kinds[0], to), send_kv(kinds[1], to)]

    def exchange(far, column, copies, act):
        def each(side, to):
            for copy in copies(2 * to + column):
                act(copy)

        beside(far, each)

    def start(copy):
        copy.start()

    def sent(copy):
        copy.wait_send()

    relay(0)
    for copy in staged:
        copy.wait()

    across = 2 * z + 1 - y
    for copy in other_column(across):
        copy.start()
    w_across = remote(w_ref, w_slot, w_send.at[0], w_recv.at[core], (across, 2 * x + y))
    w_beside = remote(w_ref, w_slot, w_send.at[1], w_recv.at[core], (me, 2 * x + y))
    w_across.start()

    @pl.when(core != y)
    def _():
        w_beside.start()

    exchange(1, y, own_column, start)
    for far in range(1, nz):
        relayed(far - 1)
        if far < nz - 1:
            relay(far)
        exchange(far, 1 - y, other_column, start)
        if far < nz - 1:
            exchange(far + 1, y, own_column, start)

    deep = nz // STEPS
    part = deep * rows
    row_id = lax.broadcasted_iota(jnp.int32, (part, 1), 0)
    row_pos = row_id + y * rows
    for index in range(1, deep):
        row_pos = row_pos + jnp.where(row_id >= index * rows, rows, 0)

    def att_part(c, source, step):
        return att.at[c * nz + source, pl.ds(step * part, part), :]

    def att_copy(source, step, send, recv, to):
        ref = att_part(core, source, step)
        return remote(ref, ref, send, recv, to)

    def along(to, step):
        return att_copy(z, step, z_send.at[to, step], z_recv.at[z, step], (2 * to + y, head))

    def forward(source, step):
        return att_copy(
            source, step, f_send.at[source, step], f_recv.at[source, step],
            (me, 2 * x + 1 - core),
        )

    for step in range(STEPS):
        for source in range(deep * step, deep * (step + 1)):
            arrived(qbuf.at[pl.ds(source * rows, rows), :], q_recv.at[source])
        for source in range(2 * deep * step, 2 * deep * (step + 1)):
            arrived(docbuf.at[source], d_recv.at[source])
            for _, dst, _, recv in kinds:
                arrived(dst.at[pl.ds(source * rows, rows), :], recv.at[source])
        seen = 2 * deep * (step + 1)
        att[core * nz + z, pl.ds(step * part, part), :] = attention(
            qbuf[step * part:(step + 1) * part, :],
            kbuf[:seen * rows, :],
            vbuf[:seen * rows, :],
            jnp.concatenate([docbuf[source] for source in range(seen)], axis=1),
            row_pos + 2 * part * step,
        )
        for far in reversed(range(1, nz)):
            beside(far, lambda side, to, step=step: along(to, step).start())
        forward(z, step).start()

    slot = 2 * x + core

    def deliver(index, act, act_own=None):
        own = (me == 2 * index + y) & (head == z)
        src = sendbuf.at[pl.ds(index * rows, rows), :]

        if act_own:
            @pl.when(own)
            def _():
                act_own(pltpu.make_async_copy(src, parts.at[slot], p_recv.at[slot]))

        @pl.when(jnp.logical_not(own))
        def _():
            act(remote(
                src, parts.at[slot], p_send.at[index], p_recv.at[slot], (2 * index + y, z)
            ))

    for step in range(STEPS):
        for far in range(1, nz):
            def pass_on(side, source, step=step):
                arrived(att_part(core, source, step), z_recv.at[source, step])
                forward(source, step).start()

            beside(far, pass_on)
        for source in range(nz):
            arrived(att_part(1 - core, source, step), f_recv.at[source, step])
        if step == 0:
            for index in range(2):
                arrived(wbuf.at[pl.ds(index * wrows, wrows), :], w_recv.at[index])
        attended = jnp.concatenate(
            [att[index, step * part:(step + 1) * part, :] for index in range(2 * nz)], axis=1
        )
        sendbuf[step * part:(step + 1) * part, :] = jnp.dot(
            attended, wbuf[...], preferred_element_type=jnp.float32
        ).astype(jnp.bfloat16)
        for index in range(deep * step, deep * (step + 1)):
            deliver(index, start, start)

    res_copy.wait()
    for c in range(2):
        for p in range(2):
            arrived(parts.at[2 * p + c], p_recv.at[2 * p + c])
        cols = slice(c * wcols, (c + 1) * wcols)
        total = parts[c].astype(jnp.float32) + parts[2 + c].astype(jnp.float32)
        out_ref[:, cols] = (resbuf[:, cols].astype(jnp.float32) + total).astype(jnp.bfloat16)

    for copy in other_column(across):
        copy.wait_send()
    w_across.wait_send()

    @pl.when(core != y)
    def _():
        w_beside.wait_send()

    for far in range(1, nz):
        exchange(far, y, own_column, sent)
        exchange(far, 1 - y, other_column, sent)
        for step in range(STEPS):
            beside(far, lambda side, to, step=step: along(to, step).wait_send())
    for step in range(STEPS):
        for source in range(nz):
            forward(source, step).wait_send()
    for index in range(nz):
        deliver(index, sent)


def fused(n, query, key_states, value_states, doc_ids, out_weight, residual):
    rows, width = key_states.shape
    wrows, wcols = out_weight.shape
    seq, nz = n * rows, n // 2
    dma = pltpu.SemaphoreType.DMA
    any_ = pl.BlockSpec(memory_space=pl.ANY)
    bf16 = jnp.bfloat16
    return pl.pallas_call(
        functools.partial(fused_kernel, nz),
        out_shape=jax.ShapeDtypeStruct(residual.shape, residual.dtype),
        in_specs=[any_] * 6,
        out_specs=pl.BlockSpec(memory_space=pltpu.VMEM),
        scratch_shapes=[
            pltpu.VMEM((rows, width), bf16),
            pltpu.VMEM((rows, width), bf16),
            pltpu.VMEM((rows, width), bf16),
            pltpu.VMEM((1, rows), jnp.int32),
            pltpu.VMEM((seq // 2, HEAD_DIM), bf16),
            pltpu.VMEM((seq, HEAD_DIM), bf16),
            pltpu.VMEM((seq, HEAD_DIM), bf16),
            pltpu.VMEM((n, 1, rows), jnp.int32),
            pltpu.VMEM((n, seq // 2, HEAD_DIM), bf16),
            pltpu.VMEM((2 * wrows, wcols), bf16),
            pltpu.VMEM((seq // 2, wcols), bf16),
            pltpu.VMEM((4, rows, wcols), bf16),
            pltpu.VMEM(residual.shape, bf16),
            dma((4,)),
            dma((n,)), dma((nz,)),
            dma((n,)), dma((n,)),
            dma((n,)), dma((n,)),
            dma((n,)), dma((n,)),
            dma((nz, STEPS)), dma((nz, STEPS)),
            dma((nz, STEPS)), dma((nz, STEPS)),
            dma((nz,)), dma((4,)),
            dma((2,)), dma((2,)), dma,
            pltpu.SemaphoreType.REGULAR((nz - 1, 2)),
        ],
        compiler_params=pltpu.CompilerParams(collective_id=0, has_side_effects=True),
    )(query, key_states, value_states, doc_ids.reshape(1, rows), out_weight, residual)


def solution(mesh):
    placed = (
        P("seq", "head"),
        P("seq", "head"),
        P("seq", "head"),
        P("seq"),
        P("head", "seq"),
        P("seq", "head"),
    )
    n, nh = mesh.shape["seq"], mesh.shape["head"]

    def body(query, key_states, value_states, doc_ids, out_weight, residual):
        heads = query.shape[1] // HEAD_DIM
        fits = (
            n == 2 * heads
            and n == 2 * nh
            and nh == 4
            and out_weight.shape[1] % 256 == 0
            and query.shape[0] % 16 == 0
        )
        run = functools.partial(fused, n) if fits else shards
        return run(query, key_states, value_states, doc_ids, out_weight, residual)

    return jax.shard_map(
        body, mesh=mesh, in_specs=placed, out_specs=P("seq", "head"), check_vma=False
    )
```

time: 40 us -> 32.3 us (0.81)
  Pallas kernels: 38.3 us -> 30.6 us
    pallas_call x1, Pallas kernels: 38.3 us -> 30.6 us  [fused(): pl.pallas_call(functools.partial(fused_kernel, nz), out_shape=jax.ShapeDt...]
where the time goes in v1:
time: 32.3 us; the launch traced here: 32.2 us
  Pallas kernels  30.6 us (95%)
  local copies, waits for them, and re-layouts  1.57 us (5%)
    pallas_call x1, Pallas kernels, fused(): pl.pallas_call(functools.partial(fused_kernel, nz), out_shape=jax.ShapeDt...  30.6 us
    unnamed x1, local copies, waits for them, and re-layouts  1.57 us

profile of v1, /device:TPU:25, one launch (start us, length us, event | category | flops | bytes accessed | tf_op | source)
XLA Modules:
  0.0 32.2 jit_solution(8567047533559363749)
XLA Ops:
  0.0 30.6 %shard_map.64 = bf16[64,1024]{1,0:T(8,128)(2,1)} custom-call(bf16[64,512]{1,0:T(8,128)(2,1)} %q_ref.1, bf16[64,512]{1,0:T(8,128)(2,1)} %k_ref.1, bf16[64,512]{1,0:T(8,128)(2,1)} %v_ref.1, s32[1,64]{1,0:T(1,128)} %bitcast.1, bf16[512,512]{1,0:T(8,128)(2,1)} %w_ref.1, bf16[64,1024]{1,0:T(8,128)(2,1)} %res_ref.1), custom_call_target="tpu_custom_call" | custom-call | tf_op jit(solution)/shard_map/pallas_call | solution.py:365
  30.6 1.6 %copy.8 = bf16[64,1024]{1,0:T(8,128)(2,1)} copy(bf16[64,1024]{1,0:T(8,128)(2,1)} %shard_map.64) | data formatting | bytes 262144

commit v2 on v1

v2 whole, which is shorter than its diff:
```python
import functools

import jax
import jax.numpy as jnp
from jax import lax
from jax.experimental import pallas as pl
from jax.experimental.pallas import tpu as pltpu
from jax.sharding import PartitionSpec as P

HEAD_DIM = 128


masked_score = -1e30


def to_heads(block):
    return block.reshape(block.shape[0], block.shape[1] // HEAD_DIM, HEAD_DIM)


def attend_block(state, queries, query_pos, query_docs, keys, values, key_pos, key_docs):
    run_max, run_sum, run_acc = state
    scores = jnp.einsum(
        "qhd,khd->hqk", queries, keys, preferred_element_type=jnp.float32
    ) * HEAD_DIM ** (-0.5)
    allowed = (key_pos[None, :] <= query_pos[:, None]) & (key_docs[None, :] == query_docs[:, None])
    scores = jnp.where(allowed[None], scores, masked_score)
    new_max = jnp.maximum(run_max, jnp.max(scores, axis=-1))
    weights = jnp.where(allowed[None], jnp.exp(scores - new_max[..., None]), 0.0)
    run_sum = jnp.sum(weights, axis=-1)
    run_acc = jnp.einsum(
        "hqk,khd->hqd", weights.astype(jnp.bfloat16), values, preferred_element_type=jnp.float32
    )
    return (new_max, run_sum, run_acc)


def shards(query, key_states, value_states, doc_ids, out_weight, residual):
    tok_rows = query.shape[0]
    heads = query.shape[1] // HEAD_DIM
    shard_index = lax.axis_index("seq")
    first_pos = shard_index * tok_rows
    groups = [(query, first_pos + jnp.arange(tok_rows, dtype=jnp.int32), doc_ids)]
    prepared = [(to_heads(block), block_pos, block_docs) for block, block_pos, block_docs in groups]
    initial = tuple(
        (
            (
                jnp.full((heads, block_pos.shape[0]), masked_score, jnp.float32),
                jnp.zeros((heads, block_pos.shape[0]), jnp.float32),
                jnp.zeros((heads, block_pos.shape[0], HEAD_DIM), jnp.float32),
            )
            for block, block_pos, block_docs in groups
        )
    )
    first_row = jnp.int32(0)
    keys = lax.all_gather(key_states, "seq", axis=0, tiled=True)
    values = lax.all_gather(value_states, "seq", axis=0, tiled=True)
    key_docs = lax.all_gather(doc_ids, "seq", axis=0, tiled=True)
    key_pos = jnp.arange(keys.shape[0], dtype=jnp.int32)
    key_heads = to_heads(keys)
    value_heads = to_heads(values)
    updated = []
    for member, state in zip(prepared, initial):
        queries, query_pos, query_docs = member

        def advance(inner, queries=queries, query_pos=query_pos, query_docs=query_docs):
            return attend_block(
                inner, queries, query_pos, query_docs, key_heads, value_heads, key_pos, key_docs
            )

        def unchanged(inner):
            return inner

        updated.append(lax.cond(first_row <= jnp.max(query_pos), advance, unchanged, state))
    finals = tuple(updated)
    outputs = []
    for run_max, run_sum, run_acc in finals:
        normed = run_acc / run_sum[..., None]
        outputs.append(
            jnp.transpose(normed, (1, 0, 2))
            .reshape(normed.shape[1], heads * HEAD_DIM)
            .astype(jnp.bfloat16)
        )
    attended = outputs[0]
    mapped = jnp.dot(
        attended,
        lax.all_gather(out_weight, "seq", axis=1, tiled=True),
        preferred_element_type=jnp.float32,
    )
    summed = lax.psum_scatter(mapped, "head", scatter_dimension=1, tiled=True)
    return (residual.astype(jnp.float32) + summed).astype(jnp.bfloat16)


MESH = pl.DeviceIdType.MESH


STEPS = 2
PIECES = 4


def attention(queries, keys, values, doc_row, row_pos):
    rows, keep = queries.shape[0], keys.shape[0]
    scores = lax.dot_general(
        queries, keys, (((1,), (1,)), ((), ())), preferred_element_type=jnp.float32
    ) * HEAD_DIM ** (-0.5)
    col_pos = lax.broadcasted_iota(jnp.int32, (rows, keep), 1)
    docs = jnp.broadcast_to(doc_row, (rows, keep))
    query_docs = jnp.sum(jnp.where(row_pos == col_pos, docs, 0.0), axis=1, keepdims=True)
    allowed = (col_pos <= row_pos) & (docs == query_docs)
    scores = jnp.where(allowed, scores, masked_score)
    row_max = jnp.max(scores, axis=1, keepdims=True)
    weights = jnp.where(allowed, jnp.exp(scores - row_max), 0.0)
    row_sum = jnp.sum(weights, axis=1, keepdims=True)
    product = jnp.dot(weights.astype(jnp.bfloat16), values, preferred_element_type=jnp.float32)
    return (product / row_sum).astype(jnp.bfloat16)


def fused_kernel(
    nz, q_ref, k_ref, v_ref, doc_ref, w_ref, res_ref, out_ref,
    stage, docin, inbox, mine, att, wbuf, sendbuf, parts, resbuf,
    in_sem, i_send, i_recv, b_send, b_recv, z_send, z_recv, f_send, f_recv,
    p_send, p_recv, w_send, w_recv, res_sem,
):
    me = lax.axis_index("seq")
    head = lax.axis_index("head")
    rows = k_ref.shape[0]
    z, y = me // 2, me % 2
    x, core = head // 2, head % 2
    wrows = w_ref.shape[0]
    wcols = w_ref.shape[1]

    tall = stage.shape[0]
    chunk = wrows // PIECES

    def peer(to):
        return 2 * to + y, head

    def greet(to):
        pl.semaphore_signal(barrier, inc=1, device_id=to, device_id_type=MESH)

    barrier = pltpu.get_barrier_semaphore()
    for dz in range(1, nz):
        greet(peer(lax.rem(z + dz, nz)))
    for dy in range(2):
        for dh in range(4):
            if dy or dh:
                greet((2 * z + lax.rem(y + dy, 2), lax.rem(head + dh, 4)))

    def arrived(ref, sem):
        pltpu.make_async_copy(ref, ref, sem).wait()

    staged = [
        pltpu.make_async_copy(src, dst, in_sem.at[index])
        for index, (src, dst) in enumerate((
            (doc_ref, docin),
            (q_ref, stage.at[pl.ds(0, rows), :]),
            (k_ref, stage.at[pl.ds(rows, rows), :]),
            (v_ref, stage.at[pl.ds(2 * rows, rows), :]),
        ))
    ]
    for copy in staged:
        copy.start()
    res_copy = pltpu.make_async_copy(res_ref, resbuf, res_sem)
    res_copy.start()

    def remote(src, dst, send, recv, to):
        return pltpu.make_async_remote_copy(
            src_ref=src, dst_ref=dst, send_sem=send, recv_sem=recv,
            device_id=to, device_id_type=MESH,
        )

    def start(copy):
        copy.start()

    def sent(copy):
        copy.wait_send()

    def by_distance(act, far_first=False):
        order = [(0, 0)] + [(far, step) for far in range(1, nz) for step in (far, -far)]
        for far, step in reversed(order) if far_first else order:
            @pl.when((z + step >= 0) & (z + step < nz))
            def _(step=step):
                act(z + step)

    def to_peer(to, src, dst, send, recv, act, act_own):
        own = to == z

        @pl.when(jnp.logical_not(own))
        def _():
            act(remote(src, dst, send, recv, peer(to)))

        if act_own:
            @pl.when(own)
            def _():
                act_own(pltpu.make_async_copy(src, dst, recv))

    partner = (me, 2 * x + 1 - core)

    def hand_out(to, act, act_own=None):
        lanes = pl.ds(pl.multiple_of(to * HEAD_DIM, HEAD_DIM), HEAD_DIM)
        to_peer(
            to, stage.at[:, lanes], inbox.at[me], i_send.at[to], i_recv.at[z], act, act_own
        )

    def share(source):
        ref = inbox.at[2 * source + y, pl.ds(rows, tall - rows), :]
        return remote(
            ref, ref, b_send.at[source], b_recv.at[source], (2 * z + 1 - y, head)
        )

    staged[0].wait()
    numbers = jnp.broadcast_to(docin[...].astype(jnp.float32), (tall - 3 * rows, rows))
    if rows < HEAD_DIM:
        blank = jnp.zeros((tall - 3 * rows, HEAD_DIM - rows), jnp.float32)
        numbers = jnp.concatenate([numbers, blank], axis=1)
    for index in range(nz):
        stage[3 * rows:, index * HEAD_DIM:(index + 1) * HEAD_DIM] = numbers.astype(jnp.bfloat16)
    for copy in staged[1:]:
        copy.wait()

    def w_part(piece):
        src = w_ref.at[pl.ds(piece * chunk, chunk), :]
        dst = wbuf.at[pl.ds(pl.multiple_of(core * wrows + piece * chunk, chunk), chunk), :]
        recv = w_recv.at[core, piece]
        return (
            pltpu.make_async_copy(src, dst, recv),
            remote(src, dst, w_send.at[0, piece], recv, (2 * z + 1 - y, 2 * x + y)),
            remote(src, dst, w_send.at[1, piece], recv, (me, 2 * x + y)),
        )

    def w_start(piece):
        kept, across, beside = w_part(piece)
        across.start()

        @pl.when(core == y)
        def _():
            kept.start()

        @pl.when(core != y)
        def _():
            beside.start()

    pl.semaphore_wait(barrier, nz + 6)

    by_distance(lambda to: hand_out(to, start, start))
    w_start(0)

    deep = nz // STEPS
    part = deep * rows
    row_id = lax.broadcasted_iota(jnp.int32, (part, 1), 0)
    row_pos = row_id + y * rows
    for index in range(1, deep):
        row_pos = row_pos + jnp.where(row_id >= index * rows, rows, 0)

    def att_part(c, source, step):
        return att.at[c * nz + source, pl.ds(step * part, part), :]

    def along(to, step, act, act_own=None):
        to_peer(
            to, mine.at[pl.ds(step * part, part), :], att_part(core, z, step),
            z_send.at[to, step], z_recv.at[z, step], act, act_own,
        )

    def forward(source, step):
        ref = att_part(core, source, step)
        return remote(ref, ref, f_send.at[source, step], f_recv.at[source, step], partner)

    def receive(source):
        arrived(inbox.at[2 * source + y], i_recv.at[source])
        share(source).start()

    by_distance(receive)
    for piece in range(1, 2):
        w_start(piece)

    for step in range(STEPS):
        for source in range(deep * step, deep * (step + 1)):
            arrived(
                inbox.at[2 * source + 1 - y, pl.ds(rows, tall - rows), :], b_recv.at[source]
            )
        seen = range(2 * deep * (step + 1))
        mine[step * part:(step + 1) * part, :] = attention(
            jnp.concatenate(
                [inbox[2 * k + y, :rows, :] for k in range(deep * step, deep * (step + 1))],
                axis=0,
            ),
            jnp.concatenate([inbox[source, rows:2 * rows, :] for source in seen], axis=0),
            jnp.concatenate([inbox[source, 2 * rows:3 * rows, :] for source in seen], axis=0),
            jnp.concatenate(
                [inbox[source, 3 * rows:, :].astype(jnp.float32)[:1, :rows] for source in seen],
                axis=1,
            ),
            row_pos + 2 * part * step,
        )
        by_distance(lambda to, step=step: along(to, step, start, start), far_first=True)
        if step == 0:
            for piece in range(2, 4):
                w_start(piece)

    slot = 2 * x + core

    def deliver(block, act, act_own=None):
        own = (me == 2 * block + y) & (head == z)
        src = sendbuf.at[pl.ds(block * rows, rows), :]

        if act_own:
            @pl.when(own)
            def _():
                act_own(pltpu.make_async_copy(src, parts.at[slot], p_recv.at[slot]))

        @pl.when(jnp.logical_not(own))
        def _():
            act(remote(
                src, parts.at[slot], p_send.at[block], p_recv.at[slot], (2 * block + y, z)
            ))

    def pass_on(step):
        def one(source):
            arrived(att_part(core, source, step), z_recv.at[source, step])
            forward(source, step).start()

        by_distance(one)

    pass_on(0)

    @pl.when(core != y)
    def _():
        for step in range(1, STEPS):
            pass_on(step)

    for step in range(STEPS):
        if step:
            @pl.when(core == y)
            def _(step=step):
                pass_on(step)

        for source in range(nz):
            arrived(att_part(1 - core, source, step), f_recv.at[source, step])
        if step == 0:
            for index in range(2):
                for piece in range(PIECES):
                    arrived(
                        wbuf.at[pl.ds(index * wrows + piece * chunk, chunk), :],
                        w_recv.at[index, piece],
                    )
        attended = jnp.concatenate(
            [att[index, step * part:(step + 1) * part, :] for index in range(2 * nz)], axis=1
        )
        sendbuf[step * part:(step + 1) * part, :] = jnp.dot(
            attended, wbuf[...], preferred_element_type=jnp.float32
        ).astype(jnp.bfloat16)
        for block in range(deep * step, deep * (step + 1)):
            deliver(block if step == 0 else deep * (2 * step + 1) - 1 - block, start, start)

    res_copy.wait()
    for c in range(2):
        for p in range(2):
            arrived(parts.at[2 * p + c], p_recv.at[2 * p + c])
        cols = slice(c * wcols, (c + 1) * wcols)
        total = parts[c].astype(jnp.float32) + parts[2 + c].astype(jnp.float32)
        out_ref[:, cols] = (resbuf[:, cols].astype(jnp.float32) + total).astype(jnp.bfloat16)

    by_distance(lambda to: hand_out(to, sent))
    for source in range(nz):
        share(source).wait_send()
    for piece in range(PIECES):
        _, across, beside = w_part(piece)
        across.wait_send()

        @pl.when(core != y)
        def _(beside=beside):
            beside.wait_send()

    for step in range(STEPS):
        by_distance(lambda to, step=step: along(to, step, sent))
        for source in range(nz):
            forward(source, step).wait_send()
    for block in range(nz):
        deliver(block, sent)


def fused(n, query, key_states, value_states, doc_ids, out_weight, residual):
    rows, width = key_states.shape
    wrows, wcols = out_weight.shape
    seq, nz = n * rows, n // 2
    dma = pltpu.SemaphoreType.DMA
    any_ = pl.BlockSpec(memory_space=pl.ANY)
    bf16 = jnp.bfloat16
    return pl.pallas_call(
        functools.partial(fused_kernel, nz),
        out_shape=jax.ShapeDtypeStruct(residual.shape, residual.dtype),
        in_specs=[any_] * 6,
        out_specs=pl.BlockSpec(memory_space=pltpu.VMEM),
        scratch_shapes=[
            pltpu.VMEM((3 * rows + 16, width), bf16),
            pltpu.VMEM((1, rows), jnp.int32),
            pltpu.VMEM((n, 3 * rows + 16, HEAD_DIM), bf16),
            pltpu.VMEM((seq // 2, HEAD_DIM), bf16),
            pltpu.VMEM((n, seq // 2, HEAD_DIM), bf16),
            pltpu.VMEM((2 * wrows, wcols), bf16),
            pltpu.VMEM((seq // 2, wcols), bf16),
            pltpu.VMEM((4, rows, wcols), bf16),
            pltpu.VMEM(residual.shape, bf16),
            dma((4,)),
            dma((nz,)), dma((nz,)),
            dma((nz,)), dma((nz,)),
            dma((nz, STEPS)), dma((nz, STEPS)),
            dma((nz, STEPS)), dma((nz, STEPS)),
            dma((nz,)), dma((4,)),
            dma((2, PIECES)), dma((2, PIECES)), dma,
        ],
        compiler_params=pltpu.CompilerParams(collective_id=0, has_side_effects=True),
    )(query, key_states, value_states, doc_ids.reshape(1, rows), out_weight, residual)


def solution(mesh):
    placed = (
        P("seq", "head"),
        P("seq", "head"),
        P("seq", "head"),
        P("seq"),
        P("head", "seq"),
        P("seq", "head"),
    )
    n, nh = mesh.shape["seq"], mesh.shape["head"]

    def body(query, key_states, value_states, doc_ids, out_weight, residual):
        heads = query.shape[1] // HEAD_DIM
        fits = (
            n == 2 * heads
            and n == 2 * nh
            and nh == 4
            and out_weight.shape[0] % (16 * PIECES) == 0
            and out_weight.shape[1] % 256 == 0
            and query.shape[0] % 16 == 0
            and query.shape[0] <= HEAD_DIM
        )
        run = functools.partial(fused, n) if fits else shards
        return run(query, key_states, value_states, doc_ids, out_weight, residual)

    return jax.shard_map(
        body, mesh=mesh, in_specs=placed, out_specs=P("seq", "head"), check_vma=False
    )
```

time: 32.3 us -> 30.4 us (0.941)
  the two profiles are of different devices: /device:TPU:25 before, /device:TPU:17 now
where the time goes in v2:
time: 30.4 us; the launch traced here: 30.2 us
  Pallas kernels  28.7 us (94%)
  local copies, waits for them, and re-layouts  1.57 us (5%)
    pallas_call x1, Pallas kernels, fused(): pl.pallas_call(functools.partial(fused_kernel, nz), out_shape=jax.ShapeDt...  28.7 us
    unnamed x1, local copies, waits for them, and re-layouts  1.57 us

profile of v2, /device:TPU:17, one launch (start us, length us, event | category | flops | bytes accessed | tf_op | source)
XLA Modules:
  0.0 30.2 jit_solution(577289909012002002)
XLA Ops:
  0.0 28.7 %shard_map.64 = bf16[64,1024]{1,0:T(8,128)(2,1)} custom-call(bf16[64,512]{1,0:T(8,128)(2,1)} %q_ref.1, bf16[64,512]{1,0:T(8,128)(2,1)} %k_ref.1, bf16[64,512]{1,0:T(8,128)(2,1)} %v_ref.1, s32[1,64]{1,0:T(1,128)} %bitcast.1, bf16[512,512]{1,0:T(8,128)(2,1)} %w_ref.1, bf16[64,1024]{1,0:T(8,128)(2,1)} %res_ref.1), custom_call_target="tpu_custom_call" | custom-call | tf_op jit(solution)/shard_map/pallas_call | solution.py:387
  28.7 1.6 %copy.8 = bf16[64,1024]{1,0:T(8,128)(2,1)} copy(bf16[64,1024]{1,0:T(8,128)(2,1)} %shard_map.64) | data formatting | bytes 262144

commit v3 on v2

--- a/solution.py
+++ b/solution.py
@@ -407,8 +407,8 @@
             dma((nz,)), dma((4,)),
             dma((2, PIECES)), dma((2, PIECES)), dma,
         ],
-        compiler_params=pltpu.CompilerParams(collective_id=0, has_side_effects=True),
-    )(query, key_states, value_states, doc_ids.reshape(1, rows), out_weight, residual)
+        compiler_params=pltpu.CompilerParams(collective_id=0, has_side_effects=True, vmem_limit_bytes=16 << 20),
+    )(*[pltpu.with_memory_space_constraint(a, pltpu.HBM) for a in (query, key_states, value_states, doc_ids.reshape(1, rows), out_weight, residual)])
 
 
 def solution(mesh):

time: 30.4 us -> 28.8 us (0.947)
  local copies, waits for them, and re-layouts: 1.57 us -> 0.66 us
  Pallas kernels: 28.7 us -> 28 us
    unnamed x1, local copies, waits for them, and re-layouts: 1.57 us -> 0.66 us
    pallas_call x1, Pallas kernels: 28.7 us -> 28 us  [fused(): pl.pallas_call(functools.partial(fused_kernel, nz), out_shape=jax.ShapeDt...]
where the time goes in v3:
time: 28.8 us; the launch traced here: 28.7 us
  Pallas kernels  28 us (97%)
  local copies, waits for them, and re-layouts  0.66 us (2%)
    pallas_call x1, Pallas kernels, fused(): pl.pallas_call(functools.partial(fused_kernel, nz), out_shape=jax.ShapeDt...  28 us
    unnamed x1, local copies, waits for them, and re-layouts  0.66 us

profile of v3, /device:TPU:17, one launch (start us, length us, event | category | flops | bytes accessed | tf_op | source)
XLA Modules:
  0.0 28.7 jit_solution(1480555395837842099)
XLA Ops:
  0.0 28.0 %shard_map.64 = bf16[64,1024]{1,0:T(8,128)(2,1)S(1)} custom-call(bf16[64,512]{1,0:T(8,128)(2,1)} %q_ref.1, bf16[64,512]{1,0:T(8,128)(2,1)} %k_ref.1, bf16[64,512]{1,0:T(8,128)(2,1)} %v_ref.1, s32[1,64]{1,0:T(1,128)} %bitcast.1, bf16[512,512]{1,0:T(8,128)(2,1)} %w_ref.1, bf16[64,1024]{1,0:T(8,128)(2,1)} %res_ref.1), custom_call_target="tpu_custom_call" | custom-call | tf_op jit(solution)/shard_map/pallas_call | solution.py:387
  28.0 0.7 %copy.8 = bf16[64,1024]{1,0:T(8,128)(2,1)} copy(bf16[64,1024]{1,0:T(8,128)(2,1)S(1)} %shard_map.64) | data formatting | bytes 262144

commit v4 on v3

--- a/solution.py
+++ b/solution.py
@@ -93,7 +93,8 @@
 
 
 STEPS = 2
-PIECES = 4
+PIECES = 8
+W_PLAN = ((3, 2, 3, 0), (2, 0, 2, 4))
 
 
 def attention(queries, keys, values, doc_row, row_pos):
@@ -115,8 +116,8 @@
 
 def fused_kernel(
     nz, q_ref, k_ref, v_ref, doc_ref, w_ref, res_ref, out_ref,
-    stage, docin, inbox, mine, att, wbuf, sendbuf, parts, resbuf,
-    in_sem, i_send, i_recv, b_send, b_recv, z_send, z_recv, f_send, f_recv,
+    stage, docin, inbox, docbuf, mine, att, wbuf, sendbuf, parts, resbuf,
+    in_sem, i_send, i_recv, b_send, b_recv, d_send, d_recv, e_send, e_recv, z_send, z_recv, f_send, f_recv,
     p_send, p_recv, w_send, w_recv, res_sem,
 ):
     me = lax.axis_index("seq")
@@ -196,24 +197,19 @@
 
     def hand_out(to, act, act_own=None):
         lanes = pl.ds(pl.multiple_of(to * HEAD_DIM, HEAD_DIM), HEAD_DIM)
+        to_peer(to, docin, docbuf.at[me], d_send.at[to], d_recv.at[z], act, act_own)
         to_peer(
             to, stage.at[:, lanes], inbox.at[me], i_send.at[to], i_recv.at[z], act, act_own
         )
 
-    def share(source):
+    def share(source, act):
         ref = inbox.at[2 * source + y, pl.ds(rows, tall - rows), :]
-        return remote(
-            ref, ref, b_send.at[source], b_recv.at[source], (2 * z + 1 - y, head)
-        )
-
-    staged[0].wait()
-    numbers = jnp.broadcast_to(docin[...].astype(jnp.float32), (tall - 3 * rows, rows))
-    if rows < HEAD_DIM:
-        blank = jnp.zeros((tall - 3 * rows, HEAD_DIM - rows), jnp.float32)
-        numbers = jnp.concatenate([numbers, blank], axis=1)
-    for index in range(nz):
-        stage[3 * rows:, index * HEAD_DIM:(index + 1) * HEAD_DIM] = numbers.astype(jnp.bfloat16)
-    for copy in staged[1:]:
+        numbers = docbuf.at[2 * source + y]
+        to = (2 * z + 1 - y, head)
+        act(remote(numbers, numbers, e_send.at[source], e_recv.at[source], to))
+        act(remote(ref, ref, b_send.at[source], b_recv.at[source], to))
+
+    for copy in staged:
         copy.wait()
 
     def w_part(piece):
@@ -238,10 +234,18 @@
         def _():
             beside.start()
 
+    def w_gate(stage):
+        for c, plan in enumerate(W_PLAN):
+            if plan[stage]:
+                @pl.when(core == c)
+                def _(plan=plan):
+                    for piece in range(sum(plan[:stage]), sum(plan[:stage + 1])):
+                        w_start(piece)
+
     pl.semaphore_wait(barrier, nz + 6)
 
     by_distance(lambda to: hand_out(to, start, start))
-    w_start(0)
+    w_gate(0)
 
     deep = nz // STEPS
     part = deep * rows
@@ -264,15 +268,16 @@
         return remote(ref, ref, f_send.at[source, step], f_recv.at[source, step], partner)
 
     def receive(source):
+        arrived(docbuf.at[2 * source + y], d_recv.at[source])
         arrived(inbox.at[2 * source + y], i_recv.at[source])
-        share(source).start()
+        share(source, start)
 
     by_distance(receive)
-    for piece in range(1, 2):
-        w_start(piece)
+    w_gate(1)
 
     for step in range(STEPS):
         for source in range(deep * step, deep * (step + 1)):
+            arrived(docbuf.at[2 * source + 1 - y], e_recv.at[source])
             arrived(
                 inbox.at[2 * source + 1 - y, pl.ds(rows, tall - rows), :], b_recv.at[source]
             )
@@ -285,15 +290,13 @@
             jnp.concatenate([inbox[source, rows:2 * rows, :] for source in seen], axis=0),
             jnp.concatenate([inbox[source, 2 * rows:3 * rows, :] for source in seen], axis=0),
             jnp.concatenate(
-                [inbox[source, 3 * rows:, :].astype(jnp.float32)[:1, :rows] for source in seen],
+                [docbuf[source].astype(jnp.float32) for source in seen],
                 axis=1,
             ),
             row_pos + 2 * part * step,
         )
         by_distance(lambda to, step=step: along(to, step, start, start), far_first=True)
-        if step == 0:
-            for piece in range(2, 4):
-                w_start(piece)
+        w_gate(2 + step)
 
     slot = 2 * x + core
 
@@ -360,7 +363,7 @@
 
     by_distance(lambda to: hand_out(to, sent))
     for source in range(nz):
-        share(source).wait_send()
+        share(source, sent)
     for piece in range(PIECES):
         _, across, beside = w_part(piece)
         across.wait_send()
@@ -390,9 +393,10 @@
         in_specs=[any_] * 6,
         out_specs=pl.BlockSpec(memory_space=pltpu.VMEM),
         scratch_shapes=[
-            pltpu.VMEM((3 * rows + 16, width), bf16),
+            pltpu.VMEM((3 * rows, width), bf16),
             pltpu.VMEM((1, rows), jnp.int32),
-            pltpu.VMEM((n, 3 * rows + 16, HEAD_DIM), bf16),
+            pltpu.VMEM((n, 3 * rows, HEAD_DIM), bf16),
+            pltpu.VMEM((n, 1, rows), jnp.int32),
             pltpu.VMEM((seq // 2, HEAD_DIM), bf16),
             pltpu.VMEM((n, seq // 2, HEAD_DIM), bf16),
             pltpu.VMEM((2 * wrows, wcols), bf16),
@@ -400,6 +404,8 @@
             pltpu.VMEM((4, rows, wcols), bf16),
             pltpu.VMEM(residual.shape, bf16),
             dma((4,)),
+            dma((nz,)), dma((nz,)),
+            dma((nz,)), dma((nz,)),
             dma((nz,)), dma((nz,)),
             dma((nz,)), dma((nz,)),
             dma((nz, STEPS)), dma((nz, STEPS)),

time: 28.8 us -> 28.5 us (0.990)
  Pallas kernels: 28 us -> 27.7 us
    pallas_call x1, Pallas kernels: 28 us -> 27.7 us  [fused(): pl.pallas_call(functools.partial(fused_kernel, nz), out_shape=jax.ShapeDt...]
where the time goes in v4:
time: 28.5 us; the launch traced here: 28.4 us
  Pallas kernels  27.7 us (97%)
  local copies, waits for them, and re-layouts  0.66 us (2%)
    pallas_call x1, Pallas kernels, fused(): pl.pallas_call(functools.partial(fused_kernel, nz), out_shape=jax.ShapeDt...  27.7 us
    unnamed x1, local copies, waits for them, and re-layouts  0.66 us

profile of v4, /device:TPU:17, one launch (start us, length us, event | category | flops | bytes accessed | tf_op | source)
XLA Modules:
  0.0 28.4 jit_solution(16815311826299160961)
XLA Ops:
  0.0 27.7 %shard_map.64 = bf16[64,1024]{1,0:T(8,128)(2,1)S(1)} custom-call(bf16[64,512]{1,0:T(8,128)(2,1)} %q_ref.1, bf16[64,512]{1,0:T(8,128)(2,1)} %k_ref.1, bf16[64,512]{1,0:T(8,128)(2,1)} %v_ref.1, s32[1,64]{1,0:T(1,128)} %bitcast.1, bf16[512,512]{1,0:T(8,128)(2,1)} %w_ref.1, bf16[64,1024]{1,0:T(8,128)(2,1)} %res_ref.1), custom_call_target="tpu_custom_call" | custom-call | tf_op jit(solution)/shard_map/pallas_call | solution.py:390
  27.7 0.7 %copy.8 = bf16[64,1024]{1,0:T(8,128)(2,1)} copy(bf16[64,1024]{1,0:T(8,128)(2,1)S(1)} %shard_map.64) | data formatting | bytes 262144

commit v5 on v4

--- a/solution.py
+++ b/solution.py
@@ -351,7 +351,7 @@
             attended, wbuf[...], preferred_element_type=jnp.float32
         ).astype(jnp.bfloat16)
         for block in range(deep * step, deep * (step + 1)):
-            deliver(block if step == 0 else deep * (2 * step + 1) - 1 - block, start, start)
+            deliver(block, start, start)
 
     res_copy.wait()
     for c in range(2):

time: 28.5 us -> 28.4 us (level)
  the two profiles are of different devices: /device:TPU:17 before, /device:TPU:25 now
where the time goes in v5:
time: 28.4 us; the launch traced here: 28.2 us
  Pallas kernels  27.6 us (97%)
  local copies, waits for them, and re-layouts  0.66 us (2%)
    pallas_call x1, Pallas kernels, fused(): pl.pallas_call(functools.partial(fused_kernel, nz), out_shape=jax.ShapeDt...  27.6 us
    unnamed x1, local copies, waits for them, and re-layouts  0.66 us

profile of v5, /device:TPU:25, one launch (start us, length us, event | category | flops | bytes accessed | tf_op | source)
XLA Modules:
  0.0 28.2 jit_solution(11234732764372660641)
XLA Ops:
  0.0 27.6 %shard_map.64 = bf16[64,1024]{1,0:T(8,128)(2,1)S(1)} custom-call(bf16[64,512]{1,0:T(8,128)(2,1)} %q_ref.1, bf16[64,512]{1,0:T(8,128)(2,1)} %k_ref.1, bf16[64,512]{1,0:T(8,128)(2,1)} %v_ref.1, s32[1,64]{1,0:T(1,128)} %bitcast.1, bf16[512,512]{1,0:T(8,128)(2,1)} %w_ref.1, bf16[64,1024]{1,0:T(8,128)(2,1)} %res_ref.1), custom_call_target="tpu_custom_call" | custom-call | tf_op jit(solution)/shard_map/pallas_call | solution.py:390
  27.6 0.7 %copy.8 = bf16[64,1024]{1,0:T(8,128)(2,1)} copy(bf16[64,1024]{1,0:T(8,128)(2,1)S(1)} %shard_map.64) | data formatting | bytes 262144
